TPU v7x, 32 devices: a whole 2x2x4 slice. The times are simulated.
32 devices in a mesh: batch: 4 (over y, core), tm: 2 (over x), space: 4 (over z).
Axes of the slice: x: 2, y: 2, z: 4, core: 2. Of those that a mesh axis runs over, the one named last changes fastest.
Arguments:
- clip_tokens: bfloat16 [4, 4, 32, 32, 1024], P('batch', None, 'space', 'tm'), may hold values from -6 to 6
- frame_order: int32 [4, 4], P('batch'), may hold values from 0 to 3, each once within a row
- row_reach: int32 [4, 4], P('batch', 'tm'), may hold values from 1 to 4
- spatial_gain: float32 [1024], replicated, may hold values from 0.1 to 1.9
- spatial_heads: bfloat16 [1024, 3072], replicated, may hold values from -2 to 2
- spatial_merge: bfloat16 [1024, 1024], replicated, may hold values from -0.1875 to 0.1875
- temporal_gain: float32 [1024], replicated, may hold values from 0.1 to 1.9
- temporal_heads: bfloat16 [1024, 3072], replicated, may hold values from -2 to 2
- temporal_merge: bfloat16 [1024, 1024], replicated, may hold values from -0.1875 to 0.1875
- cotangent: bfloat16 [4, 4, 32, 32, 1024], P('batch', 'tm', 'space'), may hold values from -0.059814453 to 0.059814453
Outputs:
- output: bfloat16 [4, 4, 32, 32, 1024], P('batch', 'tm', 'space')
- weight_grad: float32 [1024, 1024], P(('tm', 'space'))
Inputs may be any that keep to these rules, and one draw needn't show every extreme that they name: Each row of frame_order names every number from 0 to 3 once.
All inputs are finite; a program needn't handle non-finite values.
Results may differ from a plain program's by a relative error of at most 0.025.
Values may be sent and summed in bfloat16 or wider, within the bound.
A program may use at most 128 MiB of HBM per device.

v0:
```python
import jax
import jax.numpy as jnp
from jax import lax
from jax.sharding import PartitionSpec as P

HALO = 4
D = 1024
HEADS = 16
HEAD_DIM = 64
floor_term = 0.5


def extended(value, sides, width):
    for axis, dim in sides:
        devices, length = (lax.axis_size(axis), value.shape[dim])
        up = [(i, (i + 1) % devices) for i in range(devices - 1)]
        down = [(j, i) for i, j in up]
        last = lax.slice_in_dim(value, length - width, length, axis=dim)
        initial = lax.slice_in_dim(value, 0, width, axis=dim)
        before = lax.ppermute(last, axis, up)
        after = lax.ppermute(initial, axis, down)
        value = jnp.concatenate([before, value, after], axis=dim)
    return value


def normalize(values, gain_vector):
    widened = values.astype(jnp.float32)
    scaled = widened * lax.rsqrt(jnp.mean(widened * widened, axis=-1, keepdims=True) + floor_term)
    return (scaled * gain_vector).astype(jnp.bfloat16)


def softmax_rounded(scores, allowed):
    masked = jnp.where(allowed, scores, -1e30)
    top_score = jnp.max(masked, axis=-1, keepdims=True)
    exponent = jnp.exp(masked - top_score)
    return (exponent / jnp.sum(exponent, axis=-1, keepdims=True)).astype(jnp.bfloat16)


def temporal_attend(queries, keys_all, values_all, query_order, key_order):
    clip_count, query_frames, positions, _ = queries.shape
    key_frames = keys_all.shape[1]
    query_heads = queries.reshape(clip_count, query_frames, positions, HEADS, HEAD_DIM)
    key_heads = keys_all.reshape(clip_count, key_frames, positions, HEADS, HEAD_DIM)
    value_heads = values_all.reshape(clip_count, key_frames, positions, HEADS, HEAD_DIM)
    scores = jnp.einsum(
        "cfthd,cgthd->cthfg", query_heads, key_heads, preferred_element_type=jnp.float32
    ) * HEAD_DIM ** (-0.5)
    allowed = key_order[:, None, :] <= query_order[:, :, None]
    weights = softmax_rounded(scores, allowed[:, None, None])
    context = jnp.einsum(
        "cthfg,cgthd->cfthd", weights, value_heads, preferred_element_type=jnp.float32
    )
    return context.reshape(clip_count, query_frames, positions, D).astype(jnp.bfloat16)


def per_device(
    clip_tokens,
    frame_order,
    row_reach,
    spatial_gain,
    spatial_heads,
    spatial_merge,
    temporal_gain,
    temporal_heads,
    temporal_merge,
    cotangent,
):
    frames_here = lax.all_to_all(clip_tokens, "tm", split_axis=1, concat_axis=3, tiled=True)
    clip_count, frame_count, row_count, col_count, _ = frames_here.shape
    tokens = row_count * col_count
    normed = normalize(frames_here, spatial_gain)
    projected = jnp.dot(normed, spatial_heads, preferred_element_type=jnp.float32).astype(
        jnp.bfloat16
    )
    key_value = extended(projected[..., D:], (("space", 2),), HALO)
    extent = (row_count + 2 * HALO) * col_count
    first_row = lax.axis_index("space") * row_count
    all_rows = row_count * lax.axis_size("space")
    query_rows = first_row + jnp.arange(tokens, dtype=jnp.int32) // col_count
    key_rows = first_row - HALO + jnp.arange(extent, dtype=jnp.int32) // col_count
    inside = (key_rows >= 0) & (key_rows < all_rows)
    distance = jnp.abs(key_rows[None, :] - query_rows[:, None])

    def spatial_item(inputs):
        queries, key_pairs, reach_now = inputs
        query_heads = queries.reshape(tokens, HEADS, HEAD_DIM)
        key_heads = key_pairs[:, :D].reshape(extent, HEADS, HEAD_DIM)
        value_heads = key_pairs[:, D:].reshape(extent, HEADS, HEAD_DIM)
        scores = jnp.einsum(
            "qhd,khd->hqk", query_heads, key_heads, preferred_element_type=jnp.float32
        ) * HEAD_DIM ** (-0.5)
        allowed = inside[None, :] & (distance <= reach_now)
        weights = softmax_rounded(scores, allowed[None])
        context = jnp.einsum(
            "hqk,khd->qhd", weights, value_heads, preferred_element_type=jnp.float32
        )
        return context.reshape(tokens, D).astype(jnp.bfloat16)

    item_count = clip_count * frame_count
    spatial_context = lax.map(
        spatial_item,
        (
            projected[..., :D].reshape(item_count, tokens, D),
            key_value.reshape(item_count, extent, 2 * D),
            row_reach.reshape(item_count),
        ),
    )
    flat_input = frames_here.reshape(clip_count, frame_count, tokens, D)
    spatial_context = spatial_context.reshape(clip_count, frame_count, tokens, D)
    middle = (
        flat_input.astype(jnp.float32)
        + jnp.dot(spatial_context, spatial_merge, preferred_element_type=jnp.float32)
    ).astype(jnp.bfloat16)
    normed_two = normalize(middle, temporal_gain)
    projected_two = jnp.dot(normed_two, temporal_heads, preferred_element_type=jnp.float32).astype(
        jnp.bfloat16
    )
    regrouped = lax.all_to_all(projected_two, "tm", split_axis=2, concat_axis=1, tiled=True)
    context_all = temporal_attend(
        regrouped[..., :D],
        regrouped[..., D : 2 * D],
        regrouped[..., 2 * D :],
        frame_order,
        frame_order,
    )
    temporal_context = lax.all_to_all(context_all, "tm", split_axis=1, concat_axis=2, tiled=True)
    output = (
        middle.astype(jnp.float32)
        + jnp.dot(temporal_context, temporal_merge, preferred_element_type=jnp.float32)
    ).astype(jnp.bfloat16)
    flat_context = temporal_context.reshape(-1, D)
    flat_cotangent = cotangent.reshape(-1, D)
    own_rows = lax.psum_scatter(
        lax.dot_general(
            flat_context,
            flat_cotangent,
            (((0,), (0,)), ((), ())),
            preferred_element_type=jnp.float32,
        ).astype(jnp.bfloat16),
        ("tm", "space"),
        scatter_dimension=0,
        tiled=True,
    )
    weight_grad = lax.psum(own_rows, "batch").astype(jnp.float32)
    return (output.reshape(clip_count, frame_count, row_count, col_count, D), weight_grad)


def solution(mesh):
    in_specs = (
        P("batch", None, "space", "tm", None),
        P("batch", None),
        P("batch", "tm"),
        P(),
        P(),
        P(),
        P(),
        P(),
        P(),
        P("batch", "tm", "space", None, None),
    )
    out_specs = (P("batch", "tm", "space", None, None), P(("tm", "space"), None))
    return jax.shard_map(
        per_device, mesh=mesh, in_specs=in_specs, out_specs=out_specs, check_vma=False
    )
```

profile of v0, /device:TPU:0, one launch (start us, length us, event | category | flops | bytes accessed | tf_op | source)
XLA Modules:
  0.0 350.0 jit_solution(2444274592889547098)
XLA Ops:
  7.2 18.8 %all_to_all.42 = bf16[1,4,8,16,1024]{4,3,2,0,1:T(8,128)(2,1)S(1)} all-to-all(bf16[1,4,8,16,1024]{4,3,2,0,1:T(8,128)(2,1)} %bitcast.124), channel_id=1, replica_groups=mesh['batch'=4,'tm'=2,'space'=4] {'tm'}, dimensions={1} | all-to-all | bytes 2097152 | tf_op jit(solution)/shard_map/all_to_all | solution.py:68
  28.0 6.9 %fusion.30 = bf16[1,2,8,32,3072]{4,3,2,1,0:T(8,128)(2,1)S(1)} fusion(bf16[1024,3072]{1,0:T(8,128)(2,1)} %param.16, f32[2,8,32,1024]{3,2,1,0:T(8,128)} %bitcast.122, f32[1024]{0:T(1024)S(1)} %copy-done.8, f32[2,8,32]{2,1,0:T(8,128)S(1)} %rsqrt.20), kind=kOutput, calls=%fused_computation.36 | convolution fusion | flops 3224371200 | bytes 11540480 | tf_op jit(solution)/shard_map/dot_general | solution.py:72
  36.8 4.7 %collective-permute-start = (bf16[1,2,4,32,2048]{4,3,2,1,0:T(8,128)(2,1)}, bf16[1,2,4,32,2048]{4,3,2,1,0:T(8,128)(2,1)}, u32[]{:S(2)}, u32[]{:S(2)}) collective-permute-start(bf16[1,2,4,32,2048]{4,3,2,1,0:T(8,128)(2,1)} %get-tuple-element.133), channel_id=1, source_target_pairs={{0,1},{1,2},{2,3},{4,5},{5,6},{6,7},{8,9},{9,10},{10,11},{12,13},{... | collective-permute-start | bytes 3145736 | tf_op jit(solution)/shard_map/ppermute | solution.py:20
  46.0 16.4 %collective-permute-done = bf16[1,2,4,32,2048]{4,3,2,1,0:T(8,128)(2,1)} collective-permute-done((bf16[1,2,4,32,2048]{4,3,2,1,0:T(8,128)(2,1)}, bf16[1,2,4,32,2048]{4,3,2,1,0:T(8,128)(2,1)}, u32[]{:S(2)}, u32[]{:S(2)}) %collective-permute-start) | collective-permute-done | bytes 1048608 | tf_op jit(solution)/shard_map/ppermute | solution.py:20
  62.4 4.9 %collective-permute-done.1 = bf16[1,2,4,32,2048]{4,3,2,1,0:T(8,128)(2,1)} collective-permute-done((bf16[1,2,4,32,2048]{4,3,2,1,0:T(8,128)(2,1)S(1)}, bf16[1,2,4,32,2048]{4,3,2,1,0:T(8,128)(2,1)}, u32[]{:S(2)}, u32[]{:S(2)}) %collective-permute-start.1) | collective-permute-done | bytes 1048608 | tf_op jit(solution)/shard_map/ppermute | solution.py:21
  70.7 52.0 %while.11 = (s32[]{:T(128)}, bf16[2,256,1024]{1,2,0:T(8,128)(2,1)}, bf16[2,512,2048]{2,1,0:T(8,128)(2,1)}, s32[2]{0:T(128)S(1)}, bf16[2,256,1024]{2,1,0:T(8,128)...) while((s32[]{:T(128)}, bf16[2,256,1024]{1,2,0:T(8,128)(2,1)}, ...), condition=%wide.region_4.5_spmd.clone, body=%wide.region_1.4_spmd.clone.sunk | while | flops 550246912 | bytes 44339888 | solution.py:100
  75.3 3.9 %copy.117 = bf16[1,512,2048]{1,2,0:T(8,128)(2,1)} copy(bf16[1,512,2048]{2,1,0:T(8,128)(2,1)} %constant_dynamic-slice_fusion.4) | data formatting | bytes 4194304 | tf_op jit(solution)/shard_map/while/body/jit(dynamic_index_in_dim)/dynamic_slice | solution.py:100
  83.3 7.7 %fusion.90 = (f32[16,256]{1,0:T(8,128)S(1)}, f32[16,256,512]{2,1,0:T(8,128)}) fusion(pred[256,512]{1,0:T(8,128)(4,1)S(1)} %fusion.89, bf16[256,16,64]{0,2,1:T(8,128)(2,1)} %bitcast.111, bf16[512,16,64]{0,2,1:T(8,128)(2,1)} %bitcast.110), kind=kOutput, calls=%fused_computation.80.clone.1 | convolution fusion | flops 276824576 | bytes 10108928 | tf_op jit(solution)/shard_map/while/body/eval_jaxpr/sub | solution.py:35
  91.0 4.9 %fusion.91 = bf16[16,64,256]{2,1,0:T(8,128)(2,1)S(1)} fusion(bf16[512,16,64]{0,2,1:T(8,128)(2,1)S(1)} %bitcast.109, f32[16,256,512]{2,1,0:T(8,128)} %get-tuple-element.192, f32[16,256]{1,0:T(8,128)S(1)} %get-tuple-element.193), kind=kOutput, calls=%fused_computation.11.clone.1 | convolution fusion | flops 272891904 | bytes 9977856 | tf_op jit(solution)/shard_map/while/body/eval_jaxpr/hqk,khd->qhd/dot_general | solution.py:94
  101.3 3.9 %copy.117 = bf16[1,512,2048]{1,2,0:T(8,128)(2,1)} copy(bf16[1,512,2048]{2,1,0:T(8,128)(2,1)} %constant_dynamic-slice_fusion.4) | data formatting | bytes 4194304 | tf_op jit(solution)/shard_map/while/body/jit(dynamic_index_in_dim)/dynamic_slice | solution.py:100
  109.3 7.6 %fusion.90 = (f32[16,256]{1,0:T(8,128)S(1)}, f32[16,256,512]{2,1,0:T(8,128)}) fusion(pred[256,512]{1,0:T(8,128)(4,1)S(1)} %fusion.89, bf16[256,16,64]{0,2,1:T(8,128)(2,1)} %bitcast.111, bf16[512,16,64]{0,2,1:T(8,128)(2,1)} %bitcast.110), kind=kOutput, calls=%fused_computation.80.clone.1 | convolution fusion | flops 276824576 | bytes 10108928 | tf_op jit(solution)/shard_map/while/body/eval_jaxpr/sub | solution.py:35
  116.9 4.9 %fusion.91 = bf16[16,64,256]{2,1,0:T(8,128)(2,1)S(1)} fusion(bf16[512,16,64]{0,2,1:T(8,128)(2,1)S(1)} %bitcast.109, f32[16,256,512]{2,1,0:T(8,128)} %get-tuple-element.192, f32[16,256]{1,0:T(8,128)S(1)} %get-tuple-element.193), kind=kOutput, calls=%fused_computation.11.clone.1 | convolution fusion | flops 272891904 | bytes 9977856 | tf_op jit(solution)/shard_map/while/body/eval_jaxpr/hqk,khd->qhd/dot_general | solution.py:94
  126.9 6.6 %fusion.33 = bf16[1,2,256,3072]{3,2,1,0:T(8,128)(2,1)S(1)} fusion(bf16[1024,3072]{1,0:T(8,128)(2,1)} %param.19, bf16[2,256,1024]{2,1,0:T(8,128)(2,1)S(1)} %get-tuple-element.136, f32[1024]{0:T(1024)S(1)} %copy-done.9, f32[2,256]{1,0:T(2,128)S(1)} %add_rsqrt_fusion.1), kind=kOutput, calls=%fused_computation.37 | convolution fusion | flops 3224895488 | bytes 10491904 | tf_op jit(solution)/shard_map/dot_general | solution.py:115
  133.5 4.9 %copy.95 = bf16[1,2,256,3072]{3,1,0,2:T(2,128)(2,1)} copy(bf16[1,2,256,3072]{3,2,1,0:T(8,128)(2,1)S(1)} %fusion.33) | data formatting | bytes 6291456 | tf_op jit(solution)/shard_map/convert_element_type | solution.py:115
  138.4 5.3 %all-to-all-start.1 = ((bf16[1,2,256,3072]{3,1,0,2:T(2,128)(2,1)}), bf16[1,2,256,3072]{3,1,0,2:T(2,128)(2,1)}, u32[]{:S(2)}, u32[]{:S(2)}) async-start(bf16[1,2,256,3072]{3,1,0,2:T(2,128)(2,1)} %copy.95), calls=%async_computation.1 | async-start | bytes 6291456 | tf_op jit(solution)/shard_map/all_to_all | solution.py:118
  144.1 34.1 %all-to-all-done.1 = bf16[1,2,256,3072]{3,1,0,2:T(2,128)(2,1)} async-done(((bf16[1,2,256,3072]{3,1,0,2:T(2,128)(2,1)}), bf16[1,2,256,3072]{3,1,0,2:T(2,128)(2,1)}, u32[]{:S(2)}, u32[]{:S(2)}) %all-to-all-start.1) | async-done | bytes 3145760 | tf_op jit(solution)/shard_map/all_to_all | solution.py:118
  192.0 6.5 %fusion.64 = f32[128,16,4,4]{2,3,1,0:T(4,128)} fusion(bf16[4,128,16,64]{3,0,2,1:T(4,128)(2,1)} %copy.101, bf16[4,128,16,64]{3,0,2,1:T(4,128)(2,1)} %copy.102), kind=kOutput, calls=%fused_computation.83 | convolution fusion | flops 4194304 | bytes 2228224 | tf_op jit(solution)/shard_map/cfthd,cgthd->cthfg/dot_general | solution.py:45
  198.5 3.8 %copy.103 = f32[128,16,4,4]{0,1,3,2:T(8,128)S(1)} copy(f32[128,16,4,4]{2,3,1,0:T(4,128)} %fusion.64) | data formatting | bytes 262144 | tf_op jit(solution)/shard_map/cfthd,cgthd->cthfg/dot_general | solution.py:45
  202.5 4.3 %copy.105 = bf16[128,16,4,4]{3,2,1,0:T(4,128)(2,1)} copy(bf16[128,16,4,4]{0,1,3,2:T(8,128)(2,1)S(1)} %divide_convert_fusion.4) | data formatting | bytes 131072 | tf_op jit(solution)/shard_map/convert_element_type | solution.py:36
  211.4 5.9 %convert_bitcast_fusion = bf16[1,4,128,16,64]{4,1,3,2,0:T(4,128)(2,1)} fusion(bf16[4,128,16,64]{3,0,2,1:T(4,128)(2,1)} %copy.104, bf16[128,16,4,4]{3,2,1,0:T(4,128)(2,1)} %copy.105), kind=kOutput, calls=%fused_computation.49 | convolution fusion | flops 4718592 | bytes 2162688 | tf_op jit(solution)/shard_map/cthfg,cgthd->cfthd/dot_general | solution.py:50
  220.8 14.2 %all_to_all.43 = bf16[1,4,128,1024]{2,3,0,1:T(8,128)(2,1)} all-to-all(bf16[1,4,128,1024]{2,3,0,1:T(8,128)(2,1)S(1)} %bitcast.120), channel_id=1, replica_groups=mesh['batch'=4,'tm'=2,'space'=4] {'tm'}, dimensions={1} | all-to-all | bytes 2097152 | tf_op jit(solution)/shard_map/all_to_all | solution.py:126
  240.8 66.8 %reduce-scatter.2.cloned.1.call-done = bf16[128,1024]{1,0:T(8,128)(2,1)} async-done(((bf16[1024,1024]{1,0:T(8,128)(2,1)}), bf16[128,1024]{1,0:T(8,128)(2,1)}) %reduce-scatter.2.cloned.1.call-update) | async-done | bytes 262160 | tf_op jit(solution)/shard_map/reduce_scatter | solution.py:133
  307.7 4.1 %fusion.39 = bf16[2,256,1024]{2,1,0:T(8,128)(2,1)} fusion(bf16[2,256,1024]{2,1,0:T(8,128)(2,1)} %copy-done.12, bf16[2,256,1024]{2,1,0:T(8,128)(2,1)S(1)} %bitcast.126, bf16[1024,1024]{1,0:T(8,128)(2,1)} %param.20), kind=kOutput, calls=%fused_computation.44 | convolution fusion | flops 1075314688 | bytes 5242880 | tf_op jit(solution)/shard_map/dot_general | solution.py:129
  311.7 29.6 %all-reduce.2.cloned.1.call-done = bf16[128,1024]{1,0:T(8,128)(2,1)} async-done(((bf16[128,1024]{1,0:T(8,128)(2,1)}), bf16[128,1024]{1,0:T(8,128)(2,1)}) %all-reduce.2.cloned.1.call-update) | async-done | bytes 262160 | tf_op jit(solution)/shard_map/psum | solution.py:144
  (84 shorter events, 65.1 us)
Async XLA Ops:
  7.2 115.5 %copy-start = (bf16[1024,1024]{1,0:T(8,128)(2,1)S(1)}, bf16[1024,1024]{1,0:T(8,128)(2,1)}, u32[]{:S(2)}) copy-start(bf16[1024,1024]{1,0:T(8,128)(2,1)} %param.17) | copy-start | bytes 6291460
  26.0 2.0 copy-start.8
  34.9 1.9 copy-start.3
  36.8 25.6 %collective-permute-start = (bf16[1,2,4,32,2048]{4,3,2,1,0:T(8,128)(2,1)}, bf16[1,2,4,32,2048]{4,3,2,1,0:T(8,128)(2,1)}, u32[]{:S(2)}, u32[]{:S(2)}) collective-permute-start(bf16[1,2,4,32,2048]{4,3,2,1,0:T(8,128)(2,1)} %get-tuple-element.133), channel_id=1, source_target_pairs={{0,1},{1,2},{2,3},{4,5},{5,6},{6,7},{8,9},{9,10},{10,11},{12,13},{... | collective-permute-start | bytes 3145736 | tf_op jit(solution)/shard_map/ppermute | solution.py:20
  41.5 25.8 %collective-permute-start.1 = (bf16[1,2,4,32,2048]{4,3,2,1,0:T(8,128)(2,1)S(1)}, bf16[1,2,4,32,2048]{4,3,2,1,0:T(8,128)(2,1)}, u32[]{:S(2)}, u32[]{:S(2)}) collective-permute-start(bf16[1,2,4,32,2048]{4,3,2,1,0:T(8,128)(2,1)S(1)} %get-tuple-element.134), channel_id=1, source_target_pairs={{1,0},{2,1},{3,2},{5,4},{6,5},{7,6},{9,8},{10,9},{11,10},{13,12},{... | collective-permute-start | bytes 3145736 | tf_op jit(solution)/shard_map/ppermute | solution.py:21
  43.0 1.9 copy-start.4
  44.9 22.3 %slice-start = ((bf16[1,2,8,32,3072]{4,3,2,1,0:T(8,128)(2,1)}), bf16[1,2,8,32,2048]{4,3,2,1,0:T(8,128)(2,1)S(1)}, s32[]{:S(2)}) async-start(bf16[1,2,8,32,3072]{4,3,2,1,0:T(8,128)(2,1)} %copy-done.3), calls=%async_computation.6 | async-start | bytes 4194304 | tf_op jit(solution)/shard_map/slice | solution.py:75
  46.0 24.7 %copy-start.10 = (s32[1,2]{1,0:T(1,128)S(1)}, s32[1,2]{1,0:T(1,128)}, u32[]{:S(2)}) copy-start(s32[1,2]{1,0:T(1,128)} %param.14) | copy-start | bytes 28
  79.2 3.1 copy-start.2
  83.3 7.7 %copy-start.1 = (bf16[512,1024]{0,1:T(8,128)(2,1)S(1)}, bf16[512,1024]{0,1:T(8,128)(2,1)}, u32[]{:S(2)}) copy-start(bf16[512,1024]{0,1:T(8,128)(2,1)} %get-tuple-element.190) | copy-start | bytes 3145732 | tf_op jit(solution)/shard_map/while
  105.2 3.1 copy-start.2
  109.3 7.6 %copy-start.1 = (bf16[512,1024]{0,1:T(8,128)(2,1)S(1)}, bf16[512,1024]{0,1:T(8,128)(2,1)}, u32[]{:S(2)}) copy-start(bf16[512,1024]{0,1:T(8,128)(2,1)} %get-tuple-element.190) | copy-start | bytes 3145732 | tf_op jit(solution)/shard_map/while
  122.6 4.3 %copy-start.9 = (f32[1024]{0:T(1024)S(1)}, f32[1024]{0:T(1024)}, u32[]{:S(2)}) copy-start(f32[1024]{0:T(1024)} %param.18) | copy-start | bytes 12292
  125.9 1.0 copy-start.12
  138.4 5.6 %copy-start.11 = (s32[1,4]{1,0:T(1,128)S(1)}, s32[1,4]{1,0:T(1,128)}, u32[]{:S(2)}) copy-start(s32[1,4]{1,0:T(1,128)} %param.13) | copy-start | bytes 52
  138.4 39.8 %all-to-all-start.1 = ((bf16[1,2,256,3072]{3,1,0,2:T(2,128)(2,1)}), bf16[1,2,256,3072]{3,1,0,2:T(2,128)(2,1)}, u32[]{:S(2)}, u32[]{:S(2)}) async-start(bf16[1,2,256,3072]{3,1,0,2:T(2,128)(2,1)} %copy.95), calls=%async_computation.1 | async-start | bytes 6291456 | tf_op jit(solution)/shard_map/all_to_all | solution.py:118
  143.7 163.9 %reduce-scatter.2.cloned.1.call-start = ((), (), s32[]{:S(2)}) async-start(), calls=%async_computation.4 | async-start | bytes 2359296 | tf_op jit(solution)/shard_map/reduce_scatter | solution.py:133
  236.5 1.6 copy-start.7
  236.6 1.0 copy-start.5
  240.7 66.9 %copy-start.6 = (bf16[1,2,2,128,1024]{4,3,2,1,0:T(8,128)(2,1)S(1)}, bf16[1,2,2,128,1024]{4,3,2,1,0:T(8,128)(2,1)}, u32[]{:S(2)}) copy-start(bf16[1,2,2,128,1024]{4,3,2,1,0:T(8,128)(2,1)} %copy-done.5) | copy-start | bytes 3145732
  240.8 100.6 %all-reduce.2.cloned.1.call-start = ((), (), s32[]{:S(2)}) async-start(), calls=%async_computation.5 | async-start | bytes 524288 | tf_op jit(solution)/shard_map/psum | solution.py:144
Sparse Core Ops, SparseCore 0:
  240.9 66.6 reduce-scatter.1
  309.9 31.3 all-reduce.1
where the time goes:
time: 351 us; the launch traced here: 350 us
  waiting for transfers between devices  152 us (43%)
  local copies, waits for them, and re-layouts  70.6 us (20%)
  matrix products  60.8 us (17%)
  blocking collectives  33 us (9%)
  between operations  14.3 us (4%)
  starting transfers between devices  11.8 us (3%)
  other arithmetic  7.61 us (2%)
    reduce_scatter x1, waiting for transfers between devices, per_device(): lax.psum_scatter(lax.dot_general(flat_context, flat_cotangent, (((0,), (0...  66.8 us
    all_to_all x1, waiting for transfers between devices, per_device(): lax.all_to_all(projected_two, 'tm', split_axis=2, concat_axis=1, tiled=True)  34.1 us
    psum x1, waiting for transfers between devices, per_device(): weight_grad = lax.psum(own_rows, 'batch').astype(jnp.float32)  29.6 us
    all_to_all x1, blocking collectives, per_device(): lax.all_to_all(clip_tokens, 'tm', split_axis=1, concat_axis=3, tiled=True)  18.8 us
    dynamic_slice x10, local copies, waits for them, and re-layouts, per_device(): lax.map(spatial_item, (projected[..., :D].reshape(item_count, tokens, D),...  17.4 us
    ppermute x1, waiting for transfers between devices, extended(): before = lax.ppermute(last, axis, up)  16.4 us
    sub x2, matrix products, softmax_rounded(): exponent = jnp.exp(masked - top_score)  15.3 us
    all_to_all x1, blocking collectives, per_device(): lax.all_to_all(context_all, 'tm', split_axis=1, concat_axis=2, tiled=True)  14.2 us
  transfers between devices with their start and end apart: 5, of which 5 were waited for; matrix products, arithmetic and copies ran while one was open for 2% of the time, Pallas kernels for 0%

commit v1 on v0

--- a/solution.py
+++ b/solution.py
@@ -141,7 +141,7 @@
         scatter_dimension=0,
         tiled=True,
     )
-    weight_grad = lax.psum(own_rows, "batch").astype(jnp.float32)
+    weight_grad = jnp.sum(lax.all_gather(own_rows, "batch"), axis=0).astype(jnp.float32)
     return (output.reshape(clip_count, frame_count, row_count, col_count, D), weight_grad)
 
 

time: 351 us -> 335 us (0.954)
  waiting for transfers between devices: 152 us -> 135 us
    psum x1 -> x0, waiting for transfers between devices: 29.6 us -> none  [per_device(): weight_grad = lax.psum(own_rows, 'batch').astype(jnp.float32)]
    all_gather x0 -> x1, waiting for transfers between devices: none -> 13.2 us  [per_device(): lax.all_gather(own_rows, 'batch')]
where the time goes in v1:
time: 335 us; the launch traced here: 334 us
  waiting for transfers between devices  135 us (40%)
  local copies, waits for them, and re-layouts  70.6 us (21%)
  matrix products  60.8 us (18%)
  blocking collectives  33 us (10%)
  between operations  14.3 us (4%)
  starting transfers between devices  11.8 us (4%)
  other arithmetic  8.09 us (2%)
    reduce_scatter x1, waiting for transfers between devices, per_device(): lax.psum_scatter(lax.dot_general(flat_context, flat_cotangent, (((0,), (0...  66.8 us
    all_to_all x1, waiting for transfers between devices, per_device(): lax.all_to_all(projected_two, 'tm', split_axis=2, concat_axis=1, tiled=True)  34.1 us
    all_to_all x1, blocking collectives, per_device(): lax.all_to_all(clip_tokens, 'tm', split_axis=1, concat_axis=3, tiled=True)  18.8 us
    dynamic_slice x10, local copies, waits for them, and re-layouts, per_device(): lax.map(spatial_item, (projected[..., :D].reshape(item_count, tokens, D),...  17.4 us
    ppermute x1, waiting for transfers between devices, extended(): before = lax.ppermute(last, axis, up)  16.4 us
    sub x2, matrix products, softmax_rounded(): exponent = jnp.exp(masked - top_score)  15.3 us
    all_to_all x1, blocking collectives, per_device(): lax.all_to_all(context_all, 'tm', split_axis=1, concat_axis=2, tiled=True)  14.2 us
    all_gather x1, waiting for transfers between devices, per_device(): lax.all_gather(own_rows, 'batch')  13.2 us
  transfers between devices with their start and end apart: 5, of which 5 were waited for; matrix products, arithmetic and copies ran while one was open for 2% of the time, Pallas kernels for 0%

profile of v1, /device:TPU:0, one launch (start us, length us, event | category | flops | bytes accessed | tf_op | source)
XLA Modules:
  0.0 334.1 jit_solution(11115330257437554762)
XLA Ops:
  7.2 18.8 %all_to_all.42 = bf16[1,4,8,16,1024]{4,3,2,0,1:T(8,128)(2,1)S(1)} all-to-all(bf16[1,4,8,16,1024]{4,3,2,0,1:T(8,128)(2,1)} %bitcast.126), channel_id=1, replica_groups=mesh['batch'=4,'tm'=2,'space'=4] {'tm'}, dimensions={1} | all-to-all | bytes 2097152 | tf_op jit(solution)/shard_map/all_to_all | solution.py:68
  28.0 6.9 %fusion.30 = bf16[1,2,8,32,3072]{4,3,2,1,0:T(8,128)(2,1)S(1)} fusion(bf16[1024,3072]{1,0:T(8,128)(2,1)} %param.16, f32[2,8,32,1024]{3,2,1,0:T(8,128)} %bitcast.123, f32[1024]{0:T(1024)S(1)} %copy-done.8, f32[2,8,32]{2,1,0:T(8,128)S(1)} %rsqrt.20), kind=kOutput, calls=%fused_computation.36 | convolution fusion | flops 3224371200 | bytes 11540480 | tf_op jit(solution)/shard_map/dot_general | solution.py:72
  36.8 4.7 %collective-permute-start = (bf16[1,2,4,32,2048]{4,3,2,1,0:T(8,128)(2,1)}, bf16[1,2,4,32,2048]{4,3,2,1,0:T(8,128)(2,1)}, u32[]{:S(2)}, u32[]{:S(2)}) collective-permute-start(bf16[1,2,4,32,2048]{4,3,2,1,0:T(8,128)(2,1)} %get-tuple-element.133), channel_id=1, source_target_pairs={{0,1},{1,2},{2,3},{4,5},{5,6},{6,7},{8,9},{9,10},{10,11},{12,13},{... | collective-permute-start | bytes 3145736 | tf_op jit(solution)/shard_map/ppermute | solution.py:20
  46.0 16.4 %collective-permute-done = bf16[1,2,4,32,2048]{4,3,2,1,0:T(8,128)(2,1)} collective-permute-done((bf16[1,2,4,32,2048]{4,3,2,1,0:T(8,128)(2,1)}, bf16[1,2,4,32,2048]{4,3,2,1,0:T(8,128)(2,1)}, u32[]{:S(2)}, u32[]{:S(2)}) %collective-permute-start) | collective-permute-done | bytes 1048608 | tf_op jit(solution)/shard_map/ppermute | solution.py:20
  62.4 4.9 %collective-permute-done.1 = bf16[1,2,4,32,2048]{4,3,2,1,0:T(8,128)(2,1)} collective-permute-done((bf16[1,2,4,32,2048]{4,3,2,1,0:T(8,128)(2,1)S(1)}, bf16[1,2,4,32,2048]{4,3,2,1,0:T(8,128)(2,1)}, u32[]{:S(2)}, u32[]{:S(2)}) %collective-permute-start.1) | collective-permute-done | bytes 1048608 | tf_op jit(solution)/shard_map/ppermute | solution.py:21
  70.7 52.0 %while.11 = (s32[]{:T(128)}, bf16[2,256,1024]{1,2,0:T(8,128)(2,1)}, bf16[2,512,2048]{2,1,0:T(8,128)(2,1)}, s32[2]{0:T(128)S(1)}, bf16[2,256,1024]{2,1,0:T(8,128)...) while((s32[]{:T(128)}, bf16[2,256,1024]{1,2,0:T(8,128)(2,1)}, ...), condition=%wide.region_4.5_spmd.clone, body=%wide.region_1.4_spmd.clone.sunk | while | flops 550246912 | bytes 44339888 | solution.py:100
  75.3 3.9 %copy.117 = bf16[1,512,2048]{1,2,0:T(8,128)(2,1)} copy(bf16[1,512,2048]{2,1,0:T(8,128)(2,1)} %constant_dynamic-slice_fusion.4) | data formatting | bytes 4194304 | tf_op jit(solution)/shard_map/while/body/jit(dynamic_index_in_dim)/dynamic_slice | solution.py:100
  83.3 7.7 %fusion.90 = (f32[16,256]{1,0:T(8,128)S(1)}, f32[16,256,512]{2,1,0:T(8,128)}) fusion(pred[256,512]{1,0:T(8,128)(4,1)S(1)} %fusion.89, bf16[256,16,64]{0,2,1:T(8,128)(2,1)} %bitcast.112, bf16[512,16,64]{0,2,1:T(8,128)(2,1)} %bitcast.111), kind=kOutput, calls=%fused_computation.80.clone.1 | convolution fusion | flops 276824576 | bytes 10108928 | tf_op jit(solution)/shard_map/while/body/eval_jaxpr/sub | solution.py:35
  91.0 4.9 %fusion.91 = bf16[16,64,256]{2,1,0:T(8,128)(2,1)S(1)} fusion(bf16[512,16,64]{0,2,1:T(8,128)(2,1)S(1)} %bitcast.110, f32[16,256,512]{2,1,0:T(8,128)} %get-tuple-element.192, f32[16,256]{1,0:T(8,128)S(1)} %get-tuple-element.193), kind=kOutput, calls=%fused_computation.11.clone.1 | convolution fusion | flops 272891904 | bytes 9977856 | tf_op jit(solution)/shard_map/while/body/eval_jaxpr/hqk,khd->qhd/dot_general | solution.py:94
  101.3 3.9 %copy.117 = bf16[1,512,2048]{1,2,0:T(8,128)(2,1)} copy(bf16[1,512,2048]{2,1,0:T(8,128)(2,1)} %constant_dynamic-slice_fusion.4) | data formatting | bytes 4194304 | tf_op jit(solution)/shard_map/while/body/jit(dynamic_index_in_dim)/dynamic_slice | solution.py:100
  109.3 7.6 %fusion.90 = (f32[16,256]{1,0:T(8,128)S(1)}, f32[16,256,512]{2,1,0:T(8,128)}) fusion(pred[256,512]{1,0:T(8,128)(4,1)S(1)} %fusion.89, bf16[256,16,64]{0,2,1:T(8,128)(2,1)} %bitcast.112, bf16[512,16,64]{0,2,1:T(8,128)(2,1)} %bitcast.111), kind=kOutput, calls=%fused_computation.80.clone.1 | convolution fusion | flops 276824576 | bytes 10108928 | tf_op jit(solution)/shard_map/while/body/eval_jaxpr/sub | solution.py:35
  116.9 4.9 %fusion.91 = bf16[16,64,256]{2,1,0:T(8,128)(2,1)S(1)} fusion(bf16[512,16,64]{0,2,1:T(8,128)(2,1)S(1)} %bitcast.110, f32[16,256,512]{2,1,0:T(8,128)} %get-tuple-element.192, f32[16,256]{1,0:T(8,128)S(1)} %get-tuple-element.193), kind=kOutput, calls=%fused_computation.11.clone.1 | convolution fusion | flops 272891904 | bytes 9977856 | tf_op jit(solution)/shard_map/while/body/eval_jaxpr/hqk,khd->qhd/dot_general | solution.py:94
  126.9 6.6 %fusion.33 = bf16[1,2,256,3072]{3,2,1,0:T(8,128)(2,1)S(1)} fusion(bf16[1024,3072]{1,0:T(8,128)(2,1)} %param.19, bf16[2,256,1024]{2,1,0:T(8,128)(2,1)S(1)} %get-tuple-element.136, f32[1024]{0:T(1024)S(1)} %copy-done.9, f32[2,256]{1,0:T(2,128)S(1)} %add_rsqrt_fusion.1), kind=kOutput, calls=%fused_computation.37 | convolution fusion | flops 3224895488 | bytes 10491904 | tf_op jit(solution)/shard_map/dot_general | solution.py:115
  133.5 4.9 %copy.95 = bf16[1,2,256,3072]{3,1,0,2:T(2,128)(2,1)} copy(bf16[1,2,256,3072]{3,2,1,0:T(8,128)(2,1)S(1)} %fusion.33) | data formatting | bytes 6291456 | tf_op jit(solution)/shard_map/convert_element_type | solution.py:115
  138.4 5.3 %all-to-all-start.1 = ((bf16[1,2,256,3072]{3,1,0,2:T(2,128)(2,1)}), bf16[1,2,256,3072]{3,1,0,2:T(2,128)(2,1)}, u32[]{:S(2)}, u32[]{:S(2)}) async-start(bf16[1,2,256,3072]{3,1,0,2:T(2,128)(2,1)} %copy.95), calls=%async_computation.1 | async-start | bytes 6291456 | tf_op jit(solution)/shard_map/all_to_all | solution.py:118
  144.1 34.1 %all-to-all-done.1 = bf16[1,2,256,3072]{3,1,0,2:T(2,128)(2,1)} async-done(((bf16[1,2,256,3072]{3,1,0,2:T(2,128)(2,1)}), bf16[1,2,256,3072]{3,1,0,2:T(2,128)(2,1)}, u32[]{:S(2)}, u32[]{:S(2)}) %all-to-all-start.1) | async-done | bytes 3145760 | tf_op jit(solution)/shard_map/all_to_all | solution.py:118
  192.0 6.5 %fusion.64 = f32[128,16,4,4]{2,3,1,0:T(4,128)} fusion(bf16[4,128,16,64]{3,0,2,1:T(4,128)(2,1)} %copy.101, bf16[4,128,16,64]{3,0,2,1:T(4,128)(2,1)} %copy.102), kind=kOutput, calls=%fused_computation.83 | convolution fusion | flops 4194304 | bytes 2228224 | tf_op jit(solution)/shard_map/cfthd,cgthd->cthfg/dot_general | solution.py:45
  198.5 3.8 %copy.103 = f32[128,16,4,4]{0,1,3,2:T(8,128)S(1)} copy(f32[128,16,4,4]{2,3,1,0:T(4,128)} %fusion.64) | data formatting | bytes 262144 | tf_op jit(solution)/shard_map/cfthd,cgthd->cthfg/dot_general | solution.py:45
  202.5 4.3 %copy.105 = bf16[128,16,4,4]{3,2,1,0:T(4,128)(2,1)} copy(bf16[128,16,4,4]{0,1,3,2:T(8,128)(2,1)S(1)} %divide_convert_fusion.4) | data formatting | bytes 131072 | tf_op jit(solution)/shard_map/convert_element_type | solution.py:36
  211.4 5.9 %convert_bitcast_fusion = bf16[1,4,128,16,64]{4,1,3,2,0:T(4,128)(2,1)} fusion(bf16[4,128,16,64]{3,0,2,1:T(4,128)(2,1)} %copy.104, bf16[128,16,4,4]{3,2,1,0:T(4,128)(2,1)} %copy.105), kind=kOutput, calls=%fused_computation.49 | convolution fusion | flops 4718592 | bytes 2162688 | tf_op jit(solution)/shard_map/cthfg,cgthd->cfthd/dot_general | solution.py:50
  220.8 14.2 %all_to_all.43 = bf16[1,4,128,1024]{2,3,0,1:T(8,128)(2,1)} all-to-all(bf16[1,4,128,1024]{2,3,0,1:T(8,128)(2,1)S(1)} %bitcast.121), channel_id=1, replica_groups=mesh['batch'=4,'tm'=2,'space'=4] {'tm'}, dimensions={1} | all-to-all | bytes 2097152 | tf_op jit(solution)/shard_map/all_to_all | solution.py:126
  240.8 66.8 %reduce-scatter.2.cloned.1.call-done = bf16[128,1024]{1,0:T(8,128)(2,1)} async-done(((bf16[1024,1024]{1,0:T(8,128)(2,1)}), bf16[128,1024]{1,0:T(8,128)(2,1)}) %reduce-scatter.2.cloned.1.call-update) | async-done | bytes 262160 | tf_op jit(solution)/shard_map/reduce_scatter | solution.py:133
  307.7 4.1 %fusion.39 = bf16[2,256,1024]{2,1,0:T(8,128)(2,1)} fusion(bf16[2,256,1024]{2,1,0:T(8,128)(2,1)} %copy-done.12, bf16[2,256,1024]{2,1,0:T(8,128)(2,1)S(1)} %bitcast.128, bf16[1024,1024]{1,0:T(8,128)(2,1)} %param.20), kind=kOutput, calls=%fused_computation.44 | convolution fusion | flops 1075314688 | bytes 5242880 | tf_op jit(solution)/shard_map/dot_general | solution.py:129
  311.7 13.2 %all-gather.3.cloned.1.call-done = bf16[512,1024]{1,0:T(8,128)(2,1)} async-done(((bf16[128,1024]{1,0:T(8,128)(2,1)}), bf16[512,1024]{1,0:T(8,128)(2,1)}) %all-gather.3.cloned.1.call-update) | async-done | bytes 1048592 | tf_op jit(solution)/shard_map/all_gather | solution.py:144
  (85 shorter events, 65.6 us)
Async XLA Ops:
  7.2 115.5 %copy-start = (bf16[1024,1024]{1,0:T(8,128)(2,1)S(1)}, bf16[1024,1024]{1,0:T(8,128)(2,1)}, u32[]{:S(2)}) copy-start(bf16[1024,1024]{1,0:T(8,128)(2,1)} %param.17) | copy-start | bytes 6291460
  26.0 2.0 copy-start.8
  34.9 1.9 copy-start.3
  36.8 25.6 %collective-permute-start = (bf16[1,2,4,32,2048]{4,3,2,1,0:T(8,128)(2,1)}, bf16[1,2,4,32,2048]{4,3,2,1,0:T(8,128)(2,1)}, u32[]{:S(2)}, u32[]{:S(2)}) collective-permute-start(bf16[1,2,4,32,2048]{4,3,2,1,0:T(8,128)(2,1)} %get-tuple-element.133), channel_id=1, source_target_pairs={{0,1},{1,2},{2,3},{4,5},{5,6},{6,7},{8,9},{9,10},{10,11},{12,13},{... | collective-permute-start | bytes 3145736 | tf_op jit(solution)/shard_map/ppermute | solution.py:20
  41.5 25.8 %collective-permute-start.1 = (bf16[1,2,4,32,2048]{4,3,2,1,0:T(8,128)(2,1)S(1)}, bf16[1,2,4,32,2048]{4,3,2,1,0:T(8,128)(2,1)}, u32[]{:S(2)}, u32[]{:S(2)}) collective-permute-start(bf16[1,2,4,32,2048]{4,3,2,1,0:T(8,128)(2,1)S(1)} %get-tuple-element.134), channel_id=1, source_target_pairs={{1,0},{2,1},{3,2},{5,4},{6,5},{7,6},{9,8},{10,9},{11,10},{13,12},{... | collective-permute-start | bytes 3145736 | tf_op jit(solution)/shard_map/ppermute | solution.py:21
  43.0 1.9 copy-start.4
  44.9 22.3 %slice-start = ((bf16[1,2,8,32,3072]{4,3,2,1,0:T(8,128)(2,1)}), bf16[1,2,8,32,2048]{4,3,2,1,0:T(8,128)(2,1)S(1)}, s32[]{:S(2)}) async-start(bf16[1,2,8,32,3072]{4,3,2,1,0:T(8,128)(2,1)} %copy-done.3), calls=%async_computation.6 | async-start | bytes 4194304 | tf_op jit(solution)/shard_map/slice | solution.py:75
  46.0 24.7 %copy-start.10 = (s32[1,2]{1,0:T(1,128)S(1)}, s32[1,2]{1,0:T(1,128)}, u32[]{:S(2)}) copy-start(s32[1,2]{1,0:T(1,128)} %param.14) | copy-start | bytes 28
  79.2 3.1 copy-start.2
  83.3 7.7 %copy-start.1 = (bf16[512,1024]{0,1:T(8,128)(2,1)S(1)}, bf16[512,1024]{0,1:T(8,128)(2,1)}, u32[]{:S(2)}) copy-start(bf16[512,1024]{0,1:T(8,128)(2,1)} %get-tuple-element.190) | copy-start | bytes 3145732 | tf_op jit(solution)/shard_map/while
  105.2 3.1 copy-start.2
  109.3 7.6 %copy-start.1 = (bf16[512,1024]{0,1:T(8,128)(2,1)S(1)}, bf16[512,1024]{0,1:T(8,128)(2,1)}, u32[]{:S(2)}) copy-start(bf16[512,1024]{0,1:T(8,128)(2,1)} %get-tuple-element.190) | copy-start | bytes 3145732 | tf_op jit(solution)/shard_map/while
  122.6 4.3 %copy-start.9 = (f32[1024]{0:T(1024)S(1)}, f32[1024]{0:T(1024)}, u32[]{:S(2)}) copy-start(f32[1024]{0:T(1024)} %param.18) | copy-start | bytes 12292
  125.9 1.0 copy-start.12
  138.4 5.6 %copy-start.11 = (s32[1,4]{1,0:T(1,128)S(1)}, s32[1,4]{1,0:T(1,128)}, u32[]{:S(2)}) copy-start(s32[1,4]{1,0:T(1,128)} %param.13) | copy-start | bytes 52
  138.4 39.8 %all-to-all-start.1 = ((bf16[1,2,256,3072]{3,1,0,2:T(2,128)(2,1)}), bf16[1,2,256,3072]{3,1,0,2:T(2,128)(2,1)}, u32[]{:S(2)}, u32[]{:S(2)}) async-start(bf16[1,2,256,3072]{3,1,0,2:T(2,128)(2,1)} %copy.95), calls=%async_computation.1 | async-start | bytes 6291456 | tf_op jit(solution)/shard_map/all_to_all | solution.py:118
  143.7 163.9 %reduce-scatter.2.cloned.1.call-start = ((), (), s32[]{:S(2)}) async-start(), calls=%async_computation.4 | async-start | bytes 2359296 | tf_op jit(solution)/shard_map/reduce_scatter | solution.py:133
  236.5 1.6 copy-start.7
  236.6 1.0 copy-start.5
  240.7 66.9 %copy-start.6 = (bf16[1,2,2,128,1024]{4,3,2,1,0:T(8,128)(2,1)S(1)}, bf16[1,2,2,128,1024]{4,3,2,1,0:T(8,128)(2,1)}, u32[]{:S(2)}) copy-start(bf16[1,2,2,128,1024]{4,3,2,1,0:T(8,128)(2,1)} %copy-done.5) | copy-start | bytes 3145732
  240.8 84.2 %all-gather.3.cloned.1.call-start = ((), (), s32[]{:S(2)}) async-start(), calls=%async_computation.5 | async-start | bytes 1310720 | tf_op jit(solution)/shard_map/all_gather | solution.py:144
Sparse Core Ops, SparseCore 0:
  240.9 66.6 reduce-scatter.1
  309.2 15.7 all-gather.2
